TPU v7x, 32 devices: a whole 2x2x4 slice. The times are simulated.
32 devices in a mesh: section: 2 (over core), dp: 4 (over z), tensor: 4 (over y, x).
Axes of the slice: x: 2, y: 2, z: 4, core: 2. Of those that a mesh axis runs over, the one named last changes fastest.
Arguments:
- inputs: bfloat16 [2, 512, 4096], P(None, 'dp', 'tensor'), may hold values from -6 to 6
- adapter_down: bfloat16 [2, 4096, 128], P('section', 'tensor'), may hold values from -0.09375 to 0.09375
- adapter_up: bfloat16 [2, 128, 4096], P('section', None, 'tensor'), may hold values from -0.5 to 0.5
- gains: bfloat16 [2, 4096], P('section', 'tensor'), may hold values from 0.25 to 1.75
- head: bfloat16 [4096, 128], P('tensor'), may hold values from -0.375 to 0.375
- labels: int32 [2, 512], P(None, 'dp'), may hold values from 0 to 127
- valid: int32 [2, 512], P(None, 'dp'), may hold values from 0 to 1, as said below
Outputs:
- grads_down: float32 [2, 4096, 128], P('section', 'tensor', 'dp')
- grads_up: float32 [2, 128, 4096], P('section', 'dp', 'tensor')
- grads_gain: float32 [2, 4096], P('section', 'tensor')
Inputs may be any that keep to these rules, and one draw needn't show every extreme that they name: In each microbatch the first of every 128 consecutive tokens is valid.
All inputs are finite; a program needn't handle non-finite values.
Results may differ from a plain program's by a relative error of at most 0.015.
Values may be sent and summed in bfloat16 or wider, within the bound.
A program may use at most 64 MiB of HBM per device.

v0:
```python
import jax
import jax.numpy as jnp
from jax import lax
from jax.sharding import PartitionSpec as P

D = 4096


epsilon = 1e-05


def passed_along(value, axis, by):
    size = lax.axis_size(axis)
    pairs = [(i, i + by) for i in range(size) if 0 <= i + by < size]
    return lax.ppermute(value, axis, pairs)


def store_slot(store, item, slot, active):
    previous = lax.dynamic_index_in_dim(store, slot, 0, keepdims=False)
    return lax.dynamic_update_index_in_dim(store, jnp.where(active, item, previous), slot, 0)


def layer_forward(inbound, gain_row, down_weight, up_weight):
    values = inbound.astype(jnp.float32)
    squares = jnp.sum(values * values, axis=1)
    scaled = (values * gain_row).astype(jnp.bfloat16)
    partial_proj = jnp.dot(scaled, down_weight, preferred_element_type=jnp.float32)
    share_squares, projected = (
        lax.psum_scatter(squares, "tensor", scatter_dimension=0, tiled=True),
        lax.psum_scatter(partial_proj, "tensor", scatter_dimension=0, tiled=True),
    )
    inverse = lax.rsqrt(share_squares / D + epsilon)
    hidden_share = jax.nn.silu(inverse[:, None] * projected).astype(jnp.bfloat16)
    hidden = lax.all_gather(hidden_share, "tensor", axis=0, tiled=True)
    outbound = (values + jnp.dot(hidden, up_weight, preferred_element_type=jnp.float32)).astype(
        jnp.bfloat16
    )
    return (outbound, projected, inverse, hidden)


def head_backward(final_state, head, label_row, valid_row):
    values = final_state.astype(jnp.float32)
    squares = jnp.sum(values * values, axis=1)
    partial_logit = jnp.dot(final_state, head, preferred_element_type=jnp.float32)
    squares, logit_base = lax.psum((squares, partial_logit), "tensor")
    inverse = lax.rsqrt(squares / D + epsilon)
    logits = inverse[:, None] * logit_base
    shifted = logits - jnp.max(logits, axis=1, keepdims=True)
    expo_terms = jnp.exp(shifted)
    softmax_prob = expo_terms / jnp.sum(expo_terms, axis=1, keepdims=True)
    classes = lax.broadcasted_iota(jnp.int32, logits.shape, 1)
    onehot = (classes == label_row[:, None]).astype(jnp.float32)
    cotangent = (softmax_prob - onehot) * valid_row[:, None].astype(jnp.float32)
    radial = jnp.sum(cotangent * logit_base, axis=1)
    weighted = (inverse[:, None] * cotangent).astype(jnp.bfloat16)
    back_term = lax.dot_general(
        weighted, head, (((1,), (1,)), ((), ())), preferred_element_type=jnp.float32
    )
    result = back_term - (inverse**3 / D * radial)[:, None] * values
    return result.astype(jnp.bfloat16)


def bottleneck_grad(hidden_grad, projected, inverse):
    pre_act = inverse[:, None] * projected
    sigmoid_val = jax.nn.sigmoid(pre_act)
    act_grad = hidden_grad * sigmoid_val * (1.0 + pre_act * (1.0 - sigmoid_val))
    radial = jnp.sum(act_grad * projected, axis=1)
    weighted = (inverse[:, None] * act_grad).astype(jnp.bfloat16)
    factor_row = inverse**3 / D * radial
    return (weighted, factor_row)


def layer_backward(
    cotangent, inbound, projected, inverse, hidden, gain_row, down_weight, up_weight
):
    partial_back = lax.dot_general(
        cotangent, up_weight, (((1,), (1,)), ((), ())), preferred_element_type=jnp.float32
    )
    grad_share = lax.psum_scatter(partial_back, "tensor", scatter_dimension=0, tiled=True)
    weighted_share, factor_share = bottleneck_grad(grad_share, projected, inverse)
    weighted = lax.all_gather(weighted_share, "tensor", axis=0, tiled=True)
    factor_row = lax.all_gather(factor_share, "tensor", axis=0, tiled=True)
    scaled_grad = lax.dot_general(
        weighted, down_weight, (((1,), (1,)), ((), ())), preferred_element_type=jnp.float32
    )
    values = inbound.astype(jnp.float32)
    outbound = (
        cotangent.astype(jnp.float32) + gain_row * scaled_grad - factor_row[:, None] * values
    ).astype(jnp.bfloat16)
    scaled = (values * gain_row).astype(jnp.bfloat16)
    down_grad = lax.dot_general(
        scaled, weighted, (((0,), (0,)), ((), ())), preferred_element_type=jnp.float32
    )
    up_grad = lax.dot_general(
        hidden, cotangent, (((0,), (0,)), ((), ())), preferred_element_type=jnp.float32
    )
    gain_grad = jnp.sum(scaled_grad * values, axis=0)
    return (outbound, down_grad, up_grad, gain_grad)


def local(inputs, adapter_down, adapter_up, gains, head, labels, valid):
    section_count = lax.axis_size("section")
    section_id = lax.axis_index("section")
    micro_count = inputs.shape[0]
    tick_count = micro_count + section_count - 1
    down_weight = adapter_down[0]
    up_weight = adapter_up[0]
    gain_row = gains[0].astype(jnp.float32)
    token_rows = inputs.shape[1]
    rank_width = down_weight.shape[1]
    saved_rows = token_rows // lax.axis_size("tensor")
    local_count = jnp.sum(valid.astype(jnp.float32))
    pre_scale = 1.0
    inbound_store = jnp.zeros_like(inputs)
    outbound_store = jnp.zeros_like(inputs)
    proj_store = jnp.zeros((micro_count, saved_rows, rank_width), jnp.float32)
    inverse_store = jnp.zeros((micro_count, saved_rows), jnp.float32)
    hidden_store = jnp.zeros((micro_count, token_rows, rank_width), jnp.bfloat16)
    received = jnp.zeros_like(inputs[0])
    for step_index in range(tick_count):
        micro_index = step_index - section_id
        active = (micro_index >= 0) & (micro_index < micro_count)
        clipped = jnp.clip(micro_index, 0, micro_count - 1)
        first_input = lax.dynamic_index_in_dim(inputs, clipped, 0, keepdims=False)
        inbound = jnp.where(section_id == 0, first_input, received)
        outbound, projected, inverse, hidden = layer_forward(
            inbound, gain_row, down_weight, up_weight
        )
        inbound_store = store_slot(inbound_store, inbound, clipped, active)
        outbound_store = store_slot(outbound_store, outbound, clipped, active)
        proj_store = store_slot(proj_store, projected, clipped, active)
        inverse_store = store_slot(inverse_store, inverse, clipped, active)
        hidden_store = store_slot(hidden_store, hidden, clipped, active)
        if step_index + 1 < tick_count:
            received = passed_along(outbound, "section", 1)
    down_total = jnp.zeros(down_weight.shape, jnp.float32)
    up_total = jnp.zeros(up_weight.shape, jnp.float32)
    gain_total = jnp.zeros(gain_row.shape, jnp.float32)
    back_received = jnp.zeros_like(inputs[0])
    is_last = section_id == section_count - 1
    for step_index in range(tick_count):
        micro_index = step_index - (section_count - 1 - section_id)
        active = (micro_index >= 0) & (micro_index < micro_count)
        clipped = jnp.clip(micro_index, 0, micro_count - 1)
        final_state = lax.dynamic_index_in_dim(outbound_store, clipped, 0, keepdims=False)
        label_row = lax.dynamic_index_in_dim(labels, clipped, 0, keepdims=False)
        valid_row = lax.dynamic_index_in_dim(valid, clipped, 0, keepdims=False)
        head_grad = head_backward(final_state, head, label_row, valid_row)
        cotangent = jnp.where(is_last & active, head_grad, back_received)
        saved_in = lax.dynamic_index_in_dim(inbound_store, clipped, 0, keepdims=False)
        saved_proj = lax.dynamic_index_in_dim(proj_store, clipped, 0, keepdims=False)
        saved_inverse = lax.dynamic_index_in_dim(inverse_store, clipped, 0, keepdims=False)
        saved_hidden = lax.dynamic_index_in_dim(hidden_store, clipped, 0, keepdims=False)
        outbound, down_grad, up_grad, gain_grad = layer_backward(
            cotangent,
            saved_in,
            saved_proj,
            saved_inverse,
            saved_hidden,
            gain_row,
            down_weight,
            up_weight,
        )
        factor = active.astype(jnp.float32)
        down_total = down_total + down_grad * factor
        up_total = up_total + up_grad * factor
        gain_total = gain_total + gain_grad * factor
        if step_index + 1 < tick_count:
            back_received = passed_along(outbound, "section", -1)
    down_piece, up_piece = (
        lax.psum_scatter(
            (down_total * pre_scale).astype(jnp.bfloat16), "dp", scatter_dimension=1, tiled=True
        ).astype(jnp.float32),
        lax.psum_scatter(
            (up_total * pre_scale).astype(jnp.bfloat16), "dp", scatter_dimension=0, tiled=True
        ).astype(jnp.float32),
    )
    gain_summed, count_summed = lax.psum((gain_total, local_count), "dp")
    post_scale = 1.0 / count_summed
    gain_final = gain_summed * post_scale
    return ((down_piece * post_scale)[None], (up_piece * post_scale)[None], gain_final[None])


def solution(mesh):
    return jax.shard_map(
        local,
        mesh=mesh,
        in_specs=(
            P(None, "dp", "tensor"),
            P("section", "tensor", None),
            P("section", None, "tensor"),
            P("section", "tensor"),
            P("tensor", None),
            P(None, "dp"),
            P(None, "dp"),
        ),
        out_specs=(
            P("section", "tensor", "dp"),
            P("section", "dp", "tensor"),
            P("section", "tensor"),
        ),
        check_vma=False,
    )
```

profile of v0, /device:TPU:0, one launch (start us, length us, event | category | flops | bytes accessed | tf_op | source)
XLA Modules:
  0.0 359.1 jit_solution(9906430966281404676)
XLA Ops:
  8.0 1.9 fusion.46
  10.2 11.4 %all-reduce.2 = f32[128]{0:T(128)S(1)} all-reduce(f32[128]{0:T(128)S(1)} %fusion.23), channel_id=2, replica_groups=mesh['section'=2,'dp'=4,'tensor'=4] {'tensor'}, use_global_device_ids=true, to_apply=%region_1.2.clone | all-reduce | flops 128 | bytes 1024
  26.9 11.2 %reduce-scatter.9.cloned.1.call-done = f32[32,128]{1,0:T(8,128)} async-done(((f32[128,128]{1,0:T(8,128)}), f32[32,128]{1,0:T(8,128)}) %reduce-scatter.9.cloned.1.call-update) | async-done | bytes 16400 | tf_op jit(solution)/shard_map/reduce_scatter | solution.py:30
  38.1 0.8 multiply_convert_fusion.11
  38.9 8.2 %all_gather.24 = bf16[128,128]{1,0:T(8,128)(2,1)S(1)} all-gather(bf16[32,128]{1,0:T(8,128)(2,1)S(1)} %multiply_convert_fusion.11), channel_id=1, replica_groups=mesh['section'=2,'dp'=4,'tensor'=4] {'tensor'}, dimensions={0}, use_global_device_ids=true | all-gather | bytes 40960 | tf_op jit(solution)/shard_map/all_gather | solution.py:34
  47.4 1.3 collective-permute-start
  50.5 0.9 fusion.42
  51.5 8.9 %all-reduce.3 = f32[128]{0:T(128)S(1)} all-reduce(f32[128]{0:T(128)S(1)} %fusion.26), channel_id=4, replica_groups=mesh['section'=2,'dp'=4,'tensor'=4] {'tensor'}, use_global_device_ids=true, to_apply=%region_4.5.clone | all-reduce | flops 128 | bytes 1024
  60.6 15.1 %reduce-scatter.11.cloned.1.call-done = f32[32,128]{1,0:T(8,128)} async-done(((f32[128,128]{1,0:T(8,128)}), f32[32,128]{1,0:T(8,128)}) %reduce-scatter.11.cloned.1.call-update) | async-done | bytes 16400 | tf_op jit(solution)/shard_map/reduce_scatter | solution.py:30
  75.7 0.8 multiply_convert_fusion.10
  76.5 8.1 %all_gather.25 = bf16[128,128]{1,0:T(8,128)(2,1)S(1)} all-gather(bf16[32,128]{1,0:T(8,128)(2,1)S(1)} %multiply_convert_fusion.10), channel_id=1, replica_groups=mesh['section'=2,'dp'=4,'tensor'=4] {'tensor'}, dimensions={0}, use_global_device_ids=true | all-gather | bytes 40960 | tf_op jit(solution)/shard_map/all_gather | solution.py:34
  84.9 1.3 collective-permute-start.1
  86.3 1.0 collective-permute-done.1
  87.6 0.9 fusion.40
  88.5 8.9 %all-reduce.4 = f32[128]{0:T(128)S(1)} all-reduce(f32[128]{0:T(128)S(1)} %fusion.28), channel_id=6, replica_groups=mesh['section'=2,'dp'=4,'tensor'=4] {'tensor'}, use_global_device_ids=true, to_apply=%region_7.8.clone | all-reduce | flops 128 | bytes 1024
  97.6 23.1 %reduce-scatter.13.cloned.1.call-done = f32[32,128]{1,0:T(8,128)} async-done(((f32[128,128]{1,0:T(8,128)}), f32[32,128]{1,0:T(8,128)}) %reduce-scatter.13.cloned.1.call-update) | async-done | bytes 16400 | tf_op jit(solution)/shard_map/reduce_scatter | solution.py:30
  120.7 0.8 multiply_convert_fusion.9
  121.5 8.1 %all_gather.26 = bf16[128,128]{1,0:T(8,128)(2,1)S(1)} all-gather(bf16[32,128]{1,0:T(8,128)(2,1)S(1)} %multiply_convert_fusion.9), channel_id=1, replica_groups=mesh['section'=2,'dp'=4,'tensor'=4] {'tensor'}, dimensions={0}, use_global_device_ids=true | all-gather | bytes 40960 | tf_op jit(solution)/shard_map/all_gather | solution.py:34
  130.6 0.8 fusion.50
  131.5 0.9 fusion.53
  132.3 0.8 fusion.55
  133.8 8.9 %psum.56 = f32[128]{0:T(128)S(1)} all-reduce(f32[128]{0:T(128)S(1)} %get-tuple-element.7), channel_id=1, replica_groups=mesh['section'=2,'dp'=4,'tensor'=4] {'tensor'}, use_global_device_ids=true, to_apply=%region_10.11 | all-reduce | flops 128 | bytes 1024 | tf_op jit(solution)/shard_map/psum | solution.py:45
  142.8 42.3 %all-reduce.11.cloned.1.call-done = (f32[128,128]{1,0:T(8,128)}, f32[128,128]{1,0:T(8,128)}, f32[128,128]{1,0:T(8,128)}) async-done(((f32[128,128]{1,0:T(8,128)}, f32[128,128]{1,0:T(8,128)}, f32[128,128]{1,0:T(8,128)}), (f32[128,128]{1,0:T(8,128)}, f32[128,128]{1,0:T(8,128)}, f32[128,128]{1,0:T(8,128)})) %all-reduce.11.cloned.1.call-update) | async-done | bytes 196624 | tf_op jit(solution)/shard_map/psum | solution.py:45
  185.2 1.1 multiply_reduce_fusion.5
  187.1 0.9 fusion.61
  188.6 23.8 %reduce-scatter.15.cloned.1.call-done = f32[32,128]{1,0:T(8,128)} async-done(((f32[128,128]{1,0:T(8,128)}), f32[32,128]{1,0:T(8,128)}) %reduce-scatter.15.cloned.1.call-update) | async-done | bytes 16400 | tf_op jit(solution)/shard_map/reduce_scatter | solution.py:79
  212.4 0.9 fusion.111
  213.5 8.9 %all-reduce.6 = (f32[128]{0:T(128)S(1)}, f32[128]{0:T(128)S(1)}) all-reduce(f32[128]{0:T(128)S(1)} %fusion.128, f32[128]{0:T(128)S(1)} %get-tuple-element.6), channel_id=1, replica_groups=mesh['section'=2,'dp'=4,'tensor'=4] {'tensor'}, use_global_device_ids=true, to_apply=%add | all-reduce | flops 256 | bytes 2048
  222.8 8.1 %all_gather.27 = bf16[128,128]{1,0:T(8,128)(2,1)S(1)} all-gather(bf16[32,128]{1,0:T(8,128)(2,1)S(1)} %multiply_convert_fusion.8), channel_id=1, replica_groups=mesh['section'=2,'dp'=4,'tensor'=4] {'tensor'}, dimensions={0}, use_global_device_ids=true | all-gather | bytes 40960 | tf_op jit(solution)/shard_map/all_gather | solution.py:81
  231.6 1.3 collective-permute-start.2
  233.8 1.2 collective-permute-done.2
  235.3 0.9 fusion.59
  236.5 23.9 %reduce-scatter.17.cloned.1.call-done = f32[32,128]{1,0:T(8,128)} async-done(((f32[128,128]{1,0:T(8,128)}), f32[32,128]{1,0:T(8,128)}) %reduce-scatter.17.cloned.1.call-update) | async-done | bytes 16400 | tf_op jit(solution)/shard_map/reduce_scatter | solution.py:79
  260.5 0.9 fusion.110
  261.5 9.0 %all-reduce.5 = (f32[128]{0:T(128)S(1)}, f32[128]{0:T(128)S(1)}) all-reduce(f32[128]{0:T(128)S(1)} %fusion.133, f32[128]{0:T(128)} %get-tuple-element.5), channel_id=1, replica_groups=mesh['section'=2,'dp'=4,'tensor'=4] {'tensor'}, use_global_device_ids=true, to_apply=%add.1 | all-reduce | flops 256 | bytes 2048
  271.0 8.1 %all_gather.29 = bf16[128,128]{1,0:T(8,128)(2,1)S(1)} all-gather(bf16[32,128]{1,0:T(8,128)(2,1)S(1)} %multiply_convert_fusion.7), channel_id=1, replica_groups=mesh['section'=2,'dp'=4,'tensor'=4] {'tensor'}, dimensions={0}, use_global_device_ids=true | all-gather | bytes 40960 | tf_op jit(solution)/shard_map/all_gather | solution.py:81
  279.5 1.3 collective-permute-start.3
  282.0 0.9 collective-permute-done.3
  283.2 0.9 fusion.57
  284.4 1.0 fusion.4
  285.5 22.9 %reduce-scatter.19.cloned.1.call-done = f32[32,128]{1,0:T(8,128)} async-done(((f32[128,128]{1,0:T(8,128)}), f32[32,128]{1,0:T(8,128)}) %reduce-scatter.19.cloned.1.call-update) | async-done | bytes 16400 | tf_op jit(solution)/shard_map/reduce_scatter | solution.py:79
  308.4 0.8 multiply_convert_fusion.6
  309.2 8.1 %all_gather.31 = bf16[128,128]{1,0:T(8,128)(2,1)S(1)} all-gather(bf16[32,128]{1,0:T(8,128)(2,1)S(1)} %multiply_convert_fusion.6), channel_id=1, replica_groups=mesh['section'=2,'dp'=4,'tensor'=4] {'tensor'}, dimensions={0}, use_global_device_ids=true | all-gather | bytes 40960 | tf_op jit(solution)/shard_map/all_gather | solution.py:81
  318.3 1.0 fusion.5
  319.3 12.4 %all-reduce.8 = (f32[]{:T(128)}, f32[1024]{0:T(1024)S(1)}) all-reduce(f32[]{:T(128)} %convert_reduce_fusion, f32[1024]{0:T(1024)S(1)} %multiply_add_fusion), channel_id=1, replica_groups=mesh['section'=2,'dp'=4,'tensor'=4] {'dp'}, use_global_device_ids=true, to_apply=%region_34.35 | all-reduce | flops 1025 | bytes 8200 | tf_op jit(solution)/shard_map/psum | solution.py:178
  333.0 1.5 multiply_bitcast_fusion
  334.6 16.5 %reduce-scatter.21.cloned.1.call-done = bf16[1024,32]{0,1:T(8,128)(2,1)} async-done(((bf16[1024,128]{0,1:T(8,128)(2,1)}), bf16[1024,32]{0,1:T(8,128)(2,1)}) %reduce-scatter.21.cloned.1.call-update) | async-done | bytes 65552 | tf_op jit(solution)/shard_map/reduce_scatter | solution.py:171
  351.1 1.5 multiply_bitcast_fusion.1
  (134 shorter events, 18.4 us)
Async XLA Ops:
  7.2 40.0 %copy-start = (bf16[1,128,1024]{2,1,0:T(8,128)(2,1)S(1)}, bf16[1,128,1024]{2,1,0:T(8,128)(2,1)}, u32[]{:S(2)}) copy-start(bf16[1,128,1024]{2,1,0:T(8,128)(2,1)} %param.9) | copy-start | bytes 786436
  7.2 2.8 copy-start.3
  7.2 30.9 %reduce-scatter.9.cloned.1.call-start = ((), (), s32[]{:S(2)}) async-start(), calls=%async_computation.8 | async-start | bytes 81920 | tf_op jit(solution)/shard_map/reduce_scatter | solution.py:30
  9.9 65.8 %reduce-scatter.11.cloned.1.call-start = ((), (), s32[]{:S(2)}) async-start(), calls=%async_computation.9 | async-start | bytes 81920 | tf_op jit(solution)/shard_map/reduce_scatter | solution.py:30
  21.6 0.7 copy-start.20
  23.5 0.7 copy-start.15
  24.8 0.7 copy-start.14
  47.4 2.4 collective-permute-start
  48.8 0.7 copy-start.13
  49.5 1.0 copy-start.1
  51.5 69.2 %reduce-scatter.13.cloned.1.call-start = ((), (), s32[]{:S(2)}) async-start(), calls=%async_computation.10 | async-start | bytes 81920 | tf_op jit(solution)/shard_map/reduce_scatter | solution.py:30
  84.9 1.4 copy-start.12
  84.9 2.4 collective-permute-start.1
  97.4 87.8 %all-reduce.11.cloned.1.call-start = ((), (), s32[]{:S(2)}) async-start(), calls=%async_computation.16 | async-start | bytes 393216 | tf_op jit(solution)/shard_map/psum | solution.py:45
  129.7 1.0 copy-start.2
  142.8 69.7 %reduce-scatter.15.cloned.1.call-start = ((), (), s32[]{:S(2)}) async-start(), calls=%async_computation.11 | async-start | bytes 81920 | tf_op jit(solution)/shard_map/reduce_scatter | solution.py:79
  185.2 1.1 copy-start.6
  187.9 0.7 copy-start.11
  187.9 34.4 %copy-start.5 = (f32[128,128]{1,0:T(8,128)S(1)}, f32[128,128]{1,0:T(8,128)}, u32[]{:S(2)}) copy-start(f32[128,128]{1,0:T(8,128)} %get-tuple-element.13) | copy-start | bytes 196612
  188.0 72.5 %reduce-scatter.17.cloned.1.call-start = ((), (), s32[]{:S(2)}) async-start(), calls=%async_computation.12 | async-start | bytes 81920 | tf_op jit(solution)/shard_map/reduce_scatter | solution.py:79
  188.6 34.1 %copy-start.7 = (f32[2,32,128]{2,1,0:T(8,128)}, f32[2,32,128]{2,1,0:T(8,128)S(1)}, u32[]{:S(2)}) copy-start(f32[2,32,128]{2,1,0:T(8,128)S(1)} %bitcast_dynamic-update-slice_fusion.7) | copy-start | bytes 98308
  231.0 0.6 copy-start.9
  231.6 3.4 collective-permute-start.2
  232.9 0.7 copy-start.18
  232.9 0.7 copy-start.19
  236.2 72.1 %reduce-scatter.19.cloned.1.call-start = ((), (), s32[]{:S(2)}) async-start(), calls=%async_computation.13 | async-start | bytes 81920 | tf_op jit(solution)/shard_map/reduce_scatter | solution.py:79
  236.5 34.0 %copy-start.4 = (f32[128,128]{1,0:T(8,128)S(1)}, f32[128,128]{1,0:T(8,128)}, u32[]{:S(2)}) copy-start(f32[128,128]{1,0:T(8,128)} %get-tuple-element.14) | copy-start | bytes 196612
  279.5 3.4 collective-permute-start.3
  280.8 0.6 copy-start.16
  280.8 0.7 copy-start.17
  284.1 48.9 %reduce-scatter.23.cloned.1.call-start = ((), (), s32[]{:S(2)}) async-start(), calls=%async_computation.15 | async-start | bytes 327680 | tf_op jit(solution)/shard_map/reduce_scatter | solution.py:174
  285.4 23.0 %copy-start.8 = (f32[2,32,128]{2,1,0:T(8,128)S(1)}, f32[2,32,128]{2,1,0:T(8,128)}, u32[]{:S(2)}) copy-start(f32[2,32,128]{2,1,0:T(8,128)} %copy-done.7) | copy-start | bytes 98308
  285.4 65.7 %reduce-scatter.21.cloned.1.call-start = ((), (), s32[]{:S(2)}) async-start(), calls=%async_computation.14 | async-start | bytes 327680 | tf_op jit(solution)/shard_map/reduce_scatter | solution.py:171
  317.6 0.8 copy-start.10
Sparse Core Ops, SparseCore 0:
  11.3 26.7 reduce-scatter.8
  51.6 24.0 reduce-scatter.10
  97.5 23.1 reduce-scatter.12
  142.9 42.2 all-reduce.10
  188.3 24.0 reduce-scatter.14
  236.3 24.0 reduce-scatter.16
  284.2 24.0 reduce-scatter.18
  310.6 20.0 reduce-scatter.22
  333.0 18.0 reduce-scatter.20
where the time goes:
time: 360 us; the launch traced here: 359 us
  waiting for transfers between devices  183 us (51%)
  blocking collectives  117 us (32%)
  between operations  16.4 us (5%)
  other arithmetic  15.5 us (4%)
  matrix products  14.2 us (4%)
  local copies, waits for them, and re-layouts  7.62 us (2%)
  starting transfers between devices  5.56 us (2%)
    reduce_scatter x3, waiting for transfers between devices, layer_backward(): lax.psum_scatter(partial_back, 'tensor', scatter_dimension=0, tiled=True)  70.6 us
    reduce_scatter x3, waiting for transfers between devices, layer_forward(): lax.psum_scatter(partial_proj, 'tensor', scatter_dimension=0, tiled=True)  49.5 us
    unnamed x5, blocking collectives  47.1 us
    psum x1, waiting for transfers between devices, head_backward(): squares, logit_base = lax.psum((squares, partial_logit), 'tensor')  42.3 us
    all_gather x3, blocking collectives, layer_forward(): hidden = lax.all_gather(hidden_share, 'tensor', axis=0, tiled=True)  24.4 us
    all_gather x3, blocking collectives, layer_backward(): weighted = lax.all_gather(weighted_share, 'tensor', axis=0, tiled=True)  24.4 us
    reduce_scatter x1, waiting for transfers between devices, local(): lax.psum_scatter((down_total * pre_scale).astype(jnp.bfloat16), 'dp', sca...  16.5 us
    psum x1, blocking collectives, local(): gain_summed, count_summed = lax.psum((gain_total, local_count), 'dp')  12.4 us
  transfers between devices with their start and end apart: 13, of which 12 were waited for; matrix products, arithmetic and copies ran while one was open for 3% of the time, Pallas kernels for 0%

commit v1 on v0

v1 whole, which is shorter than its diff:
```python
import functools

import jax
import jax.numpy as jnp
from jax import lax
from jax.experimental import pallas as pl
from jax.experimental.pallas import tpu as pltpu
from jax.sharding import PartitionSpec as P

MESH = pl.DeviceIdType.MESH
epsilon = 1e-05
F32 = jnp.float32
BF16 = jnp.bfloat16


def mm(a, b):
    return jnp.dot(a, b, preferred_element_type=F32)


def mm_nt(a, b):
    return lax.dot_general(a, b, (((1,), (1,)), ((), ())), preferred_element_type=F32)


def mm_tn(a, b):
    return lax.dot_general(a, b, (((0,), (0,)), ((), ())), preferred_element_type=F32)


def split(v):
    high = v.astype(BF16)
    return high, (v - high.astype(F32)).astype(BF16)


def kernel(
    nt, nd, width,
    x_ref, dn_ref, up_ref, gain_ref, head_ref, lab_ref, val_ref,
    down_out, up_out, gain_out,
    odn, oup, ogain, stok, rtok, sgram, rgram, pgram, gall, sres, res, sdp, rdp, sgn, rgn,
    sib_s, sib_r, tok_s, tok_r, gr_s, gr_r, ga_s, ga_r, re_s, re_r, dp_s, dp_r,
):
    s, d, t = lax.axis_index("section"), lax.axis_index("dp"), lax.axis_index("tensor")
    first = s == 0
    tokens, feats = x_ref.shape
    rank = dn_ref.shape[1]
    half = tokens // 2
    own = half // nt
    rows = rank // nt
    part = rank // nd
    wire = stok.dtype

    def peer(k, other):
        return (1 - s if other else s, d, lax.rem(t + k, nt))

    group = [(k, o) for k in range(nt) for o in (0, 1) if (k, o) != (0, 0)]

    barrier = pltpu.get_barrier_semaphore()
    for k, o in group:
        pl.semaphore_signal(barrier, inc=1, device_id=peer(k, o), device_id_type=MESH)
    for k in range(1, nd):
        pl.semaphore_signal(barrier, inc=1, device_id=(s, lax.rem(d + k, nd), t), device_id_type=MESH)
    pl.semaphore_wait(barrier, len(group) + nd - 1)

    def send(src, dst, ss, rs, to):
        copy = pltpu.make_async_remote_copy(
            src_ref=src, dst_ref=dst, send_sem=ss, recv_sem=rs, device_id=to, device_id_type=MESH
        )
        copy.start()
        return copy

    started = []
    sib = [
        send(a, b, sib_s.at[i], sib_r.at[i], peer(0, 1))
        for i, (a, b) in enumerate(((up_ref, oup), (dn_ref, odn), (gain_ref, ogain)))
    ]
    started += sib

    gain = gain_ref[...].astype(F32)
    up = up_ref[...]
    head = head_ref[...]
    gram_a = mm_nt(up, up)
    gram_b = mm(up, head)
    sib[0].wait_recv()
    gram_c = mm_nt(up, oup[...])
    scaled_other = (oup[...].astype(F32) * gain).astype(BF16)
    gram_d = mm(scaled_other, dn_ref[...])
    gram_c = jnp.where(first, gram_c, gram_d)
    for j, g in enumerate((gram_a, gram_b, gram_c)):
        g = g.astype(wire)
        for i in range(nt):
            sgram[i, j] = g[i * rows : (i + 1) * rows]
    gram_copies = []
    for k in range(1, nt):
        gram_copies.append(
            send(sgram.at[lax.rem(t + k, nt)], rgram.at[k], gr_s.at[k], gr_r.at[k], peer(k, 0))
        )
    started += gram_copies

    xb = x_ref[...]
    xf = xb.astype(F32)
    proj = mm((xf * gain).astype(BF16), dn_ref[...]).astype(wire)
    xup = mm_nt(xb, up).astype(wire)
    for b in range(2):
        for i in range(nt):
            at = b * half + i * own
            stok[b, i, 0] = proj[at : at + own]
            stok[b, i, 1] = xup[at : at + own]
    tok_copies = {}
    for k in range(nt):
        to = lax.rem(t + k, nt)
        tok_copies[k, 1] = send(
            stok.at[1 - s, to, pl.ds(0, 2)], rtok.at[1, k, pl.ds(0, 2)],
            tok_s.at[1, k], tok_r.at[1, k], peer(k, 1),
        )
    xm = x_ref[pl.ds(pl.multiple_of(s * half, half), half), :]
    xmf = xm.astype(F32)
    xhead = mm(xm, head)
    squares = jnp.broadcast_to(jnp.sum(xmf * xmf, axis=1, keepdims=True), (half, rank))
    hh, hl = split(xhead)
    qh, ql = split(squares)
    lane_h = lax.broadcasted_iota(jnp.int32, (half, rank), 1)
    q = jnp.where(lane_h < rank // 2, qh.astype(F32), ql.astype(F32)).astype(wire)
    hh, hl = hh.astype(wire), hl.astype(wire)
    for i in range(nt):
        stok[s, i, 2] = hh[i * own : (i + 1) * own]
        stok[s, i, 3] = hl[i * own : (i + 1) * own]
        stok[s, i, 4] = q[i * own : (i + 1) * own]
    for k in range(1, nt):
        to = lax.rem(t + k, nt)
        tok_copies[k, 0] = send(
            stok.at[s, to], rtok.at[0, k], tok_s.at[0, k], tok_r.at[0, k], peer(k, 0)
        )
    started += list(tok_copies.values())

    total = sgram[t].astype(F32)
    for k in range(1, nt):
        gram_copies[k - 1].wait_recv()
        total = total + rgram[k].astype(F32)
    total = total.astype(wire)
    pgram[...] = total
    gall[s, t] = total
    all_copies = [
        send(pgram, gall.at[s, t], ga_s.at[o, k], ga_r.at[o, k], peer(k, o)) for k, o in group
    ]
    started += all_copies

    lab = jnp.where(first, lab_ref[0:1, :], lab_ref[1:2, :])
    val = jnp.where(first, val_ref[0:1, :], val_ref[1:2, :]).astype(F32)
    labels_n = head.shape[1]
    hot_t = jnp.where(lax.broadcasted_iota(jnp.int32, (labels_n, half), 0) == lab, val, 0.0).astype(BF16)
    val_t = jnp.broadcast_to(val, (labels_n, half)).astype(BF16)
    pick = (
        lax.broadcasted_iota(jnp.int32, (own, half), 0) + t * own
        == lax.broadcasted_iota(jnp.int32, (own, half), 1)
    ).astype(F32).astype(BF16)
    onehot = mm_nt(pick, hot_t)
    validity = mm_nt(pick, val_t)
    count = jnp.sum(val_ref[...].astype(F32))

    mine = stok[s, t].astype(F32)
    for k in range(1, nt):
        tok_copies[k, 0].wait_recv()
        mine = mine + rtok[0, k].astype(F32)
    tok_copies[0, 1].wait_recv()
    theirs = rtok[1, 0, 0:2].astype(F32)
    for k in range(1, nt):
        tok_copies[k, 1].wait_recv()
        theirs = theirs + rtok[1, k, 0:2].astype(F32)
    p0 = jnp.where(first, mine[0], theirs[0])
    p1 = jnp.where(first, theirs[0], mine[0])
    v0 = jnp.where(first, mine[1], theirs[1])
    v1 = jnp.where(first, theirs[1], mine[1])
    xh = mine[2] + mine[3]
    sq0 = mine[4][:, 0:1] + mine[4][:, rank // 2 : rank // 2 + 1]

    for c in all_copies:
        c.wait_recv()

    def gram(a, j):
        return gall[a, :, j].reshape(rank, rank).astype(BF16)

    a0, b0, c0 = gram(0, 0), gram(0, 1), gram(0, 2)
    a1, b1, d1 = gram(1, 0), gram(1, 1), gram(1, 2)

    def rowsum(v):
        return jnp.sum(v, axis=1, keepdims=True)

    inv0 = lax.rsqrt(sq0 / width + epsilon)
    pre0 = inv0 * p0
    sig0 = jax.nn.sigmoid(pre0)
    h0 = (pre0 * sig0).astype(BF16)
    h0f = h0.astype(F32)
    h0a = mm(h0, a0)
    p1 = p1 + mm(h0, d1)
    s1u0 = v0 + h0a
    s1u1 = v1 + mm(h0, c0)
    base = xh + mm(h0, b0)
    sq1 = sq0 + rowsum(h0f * (v0 + s1u0))
    inv1 = lax.rsqrt(sq1 / width + epsilon)
    pre1 = inv1 * p1
    sig1 = jax.nn.sigmoid(pre1)
    h1 = (pre1 * sig1).astype(BF16)
    h1f = h1.astype(F32)
    yu1 = s1u1 + mm(h1, a1)
    yu0 = s1u0 + mm_nt(h1, c0)
    base = base + mm(h1, b1)
    sq2 = sq1 + rowsum(h1f * (s1u1 + yu1))
    inv2 = lax.rsqrt(sq2 / width + epsilon)
    logits = inv2 * base
    expo = jnp.exp(logits - jnp.max(logits, axis=1, keepdims=True))
    cot = expo / rowsum(expo) * validity - onehot
    radial = rowsum(cot * base)
    wh = (inv2 * cot).astype(BF16)
    ch = inv2 * inv2 * inv2 / width * radial
    hg1 = mm_nt(wh, b1) - ch * yu1
    act1 = hg1 * sig1 * (1.0 + pre1 * (1.0 - sig1))
    w1 = (inv1 * act1).astype(BF16)
    c1 = inv1 * inv1 * inv1 / width * rowsum(act1 * p1)
    hg0 = mm_nt(wh, b0) - ch * yu0 + mm_nt(w1, d1) - c1 * s1u0
    act0 = hg0 * sig0 * (1.0 + pre0 * (1.0 - sig0))
    w0 = (inv0 * act0).astype(BF16)

    ch_h, ch_l = split(ch)
    c1_h, c1_l = split(c1)
    lane = lax.broadcasted_iota(jnp.int32, (own, rank), 1)
    q4 = rank // 4
    coef = jnp.where(
        lane < q4, ch_h.astype(F32),
        jnp.where(lane < 2 * q4, ch_l.astype(F32), jnp.where(lane < 3 * q4, c1_h.astype(F32), c1_l.astype(F32))),
    )
    for j, v in enumerate((h0, h1, w0, w1, wh, coef)):
        v = v.astype(wire)
        sres[j] = v
        res[s, t, j] = v
    res_copies = [
        send(sres, res.at[s, t], re_s.at[o, k], re_r.at[o, k], peer(k, o)) for k, o in group
    ]
    started += res_copies
    sib[1].wait_recv()
    sib[2].wait_recv()
    for c in res_copies:
        c.wait_recv()

    def got(j):
        return res[:, :, j].reshape(tokens, res.shape[-1])

    dp_copies = []

    def piece(j, full):
        full = full.astype(BF16)
        for i in range(nd):
            sdp[i, j] = full[i * part : (i + 1) * part]

    def finish(state, own_w, own_h, cotangent):
        scaled = (state * gain).astype(BF16)
        piece(0, mm_tn(own_w, scaled))
        gain_row = jnp.sum(mm_nt(own_w, dn_ref[...]) * state, axis=0, keepdims=True)
        sgn[0:1, :] = gain_row
        sgn[1:2, :] = jnp.full((1, feats), count, F32)
        piece(1, mm_tn(own_h, cotangent().astype(BF16)))

    h0g, h1g, w1g, whg = (got(j).astype(BF16) for j in (0, 1, 3, 4))
    cg = got(5).astype(F32)
    chg = cg[:, 0:1] + cg[:, q4 : q4 + 1]
    c1g = cg[:, 2 * q4 : 2 * q4 + 1] + cg[:, 3 * q4 : 3 * q4 + 1]

    @pl.when(s == 0)
    def _():
        def cotangent():
            s1 = xf + mm(h0g, up)
            y = s1 + mm(h1g, oup[...])
            g2 = mm_nt(whg, head) - chg * y
            return g2 + ogain[...].astype(F32) * mm_nt(w1g, odn[...]) - c1g * s1

        finish(xf, got(2).astype(BF16), h0g, cotangent)

    @pl.when(s != 0)
    def _():
        s1 = xf + mm(h0g, oup[...])

        def cotangent():
            y = s1 + mm(h1g, up)
            return mm_nt(whg, head) - chg * y

        finish(s1, w1g, h1g, cotangent)

    for k in range(1, nd):
        to = (s, lax.rem(d + k, nd), t)
        dp_copies.append((
            send(sdp.at[lax.rem(d + k, nd)], rdp.at[k], dp_s.at[0, k], dp_r.at[0, k], to),
            send(sgn, rgn.at[k], dp_s.at[1, k], dp_r.at[1, k], to),
        ))
    sums = sdp[d].astype(F32)
    small = sgn[...]
    for big, little in dp_copies:
        started += [big, little]
    for k in range(1, nd):
        dp_copies[k - 1][1].wait_recv()
        small = small + rgn[k]
        dp_copies[k - 1][0].wait_recv()
        sums = sums + rdp[k].astype(F32)
    scale = 1.0 / small[1:2, :]
    gain_out[...] = small[0:1, :] * scale
    up_out[...] = sums[1] * scale
    down_out[...] = sums[0] * scale
    for c in started:
        c.wait_send()


def solution(mesh):
    nt, nd, ns = mesh.shape["tensor"], mesh.shape["dp"], mesh.shape["section"]
    assert ns == 2

    def local(inputs, down, up, gains, head, labels, valid):
        micro, per, feats = inputs.shape
        assert micro == ns
        tokens = micro * per
        rank = down.shape[2]
        own, rows, part = tokens // ns // nt, rank // nt, rank // nd
        wire = BF16 if own % 16 == 0 and rows % 16 == 0 else F32
        vmem = pl.BlockSpec(memory_space=pltpu.VMEM)
        dma = pltpu.SemaphoreType.DMA
        down_t, up_g, gain_g = pl.pallas_call(
            functools.partial(kernel, nt, nd, feats * nt),
            out_shape=(
                jax.ShapeDtypeStruct((part, feats), F32),
                jax.ShapeDtypeStruct((part, feats), F32),
                jax.ShapeDtypeStruct((1, feats), F32),
            ),
            in_specs=[vmem] * 7,
            out_specs=(vmem,) * 3,
            scratch_shapes=[
                pltpu.VMEM((feats, rank), BF16),
                pltpu.VMEM((rank, feats), BF16),
                pltpu.VMEM((1, feats), BF16),
                pltpu.VMEM((2, nt, 5, own, rank), wire),
                pltpu.VMEM((2, nt, 5, own, rank), wire),
                pltpu.VMEM((nt, 3, rows, rank), wire),
                pltpu.VMEM((nt, 3, rows, rank), wire),
                pltpu.VMEM((3, rows, rank), wire),
                pltpu.VMEM((2, nt, 3, rows, rank), wire),
                pltpu.VMEM((6, own, rank), wire),
                pltpu.VMEM((2, nt, 6, own, rank), wire),
                pltpu.VMEM((nd, 2, part, feats), BF16),
                pltpu.VMEM((nd, 2, part, feats), BF16),
                pltpu.VMEM((2, feats), F32),
                pltpu.VMEM((nd, 2, feats), F32),
                dma((3,)), dma((3,)),
                dma((2, nt)), dma((2, nt)),
                dma((nt,)), dma((nt,)),
                dma((2, nt)), dma((2, nt)),
                dma((2, nt)), dma((2, nt)),
                dma((2, nd)), dma((2, nd)),
            ],
            compiler_params=pltpu.CompilerParams(collective_id=0, has_side_effects=True),
        )(inputs.reshape(tokens, feats), down[0], up[0], gains, head, labels, valid)
        return down_t.T[None], up_g[None], gain_g

    return jax.shard_map(
        local,
        mesh=mesh,
        in_specs=(
            P(None, "dp", "tensor"),
            P("section", "tensor", None),
            P("section", None, "tensor"),
            P("section", "tensor"),
            P("tensor", None),
            P(None, "dp"),
            P(None, "dp"),
        ),
        out_specs=(
            P("section", "tensor", "dp"),
            P("section", "dp", "tensor"),
            P("section", "tensor"),
        ),
        check_vma=False,
    )
```

time: 360 us -> 40.9 us (0.11)
  waiting for transfers between devices: 183 us -> 0 us
  blocking collectives: 117 us -> 0 us
  Pallas kernels: 0 us -> 37.2 us
  between operations: 16.4 us -> 0.65 us
  other arithmetic: 15.5 us -> 0 us
  matrix products: 14.2 us -> 0 us
  starting transfers between devices: 5.56 us -> 0 us
  local copies, waits for them, and re-layouts: 7.62 us -> 2.88 us
    reduce_scatter x8 -> x0, waiting for transfers between devices: 137 us -> none  [the longest x3 70.6 us: layer_backward(): lax.psum_scatter(partial_back, 'tensor', scatter_dimension=0, tiled=True)]
    all_gather x6 -> x0, blocking collectives: 48.8 us -> none  [the longest x3 24.4 us: layer_forward(): hidden = lax.all_gather(hidden_share, 'tensor', axis=0, tiled=True)]
    unnamed x5 -> x0, blocking collectives: 47.1 us -> none
    psum x1 -> x0, waiting for transfers between devices: 42.3 us -> none  [head_backward(): squares, logit_base = lax.psum((squares, partial_logit), 'tensor')]
    pallas_call x0 -> x1, Pallas kernels: none -> 37.2 us  [local(): pl.pallas_call(functools.partial(kernel, nt, nd, feats * nt), out_shape=(...]
    psum x2 -> x0, blocking collectives: 21.3 us -> none  [the longest x1 12.4 us: local(): gain_summed, count_summed = lax.psum((gain_total, local_count), 'dp')]
    dot_general x24 -> x0, matrix products: 14.2 us -> none  [the longest x3 3.59 us: layer_forward(): jnp.dot(scaled, down_weight, preferred_element_type=jnp.float32)]
    ppermute x4 -> x0, starting transfers between devices: 5.18 us -> none  [passed_along(): return lax.ppermute(value, axis, pairs)]
  transfers between devices with their start and end apart: 13 -> 0, of which waited for: 12 -> 0; matrix products, arithmetic and copies ran while one was open for 3% -> 0% of each run, Pallas kernels for 0% -> 0%
where the time goes in v1:
time: 40.9 us; the launch traced here: 40.7 us
  Pallas kernels  37.2 us (91%)
  local copies, waits for them, and re-layouts  2.88 us (7%)
  between operations  0.65 us (2%)
    pallas_call x1, Pallas kernels, local(): pl.pallas_call(functools.partial(kernel, nt, nd, feats * nt), out_shape=(...  37.2 us
    unnamed x7, local copies, waits for them, and re-layouts  2.88 us

profile of v1, /device:TPU:0, one launch (start us, length us, event | category | flops | bytes accessed | tf_op | source)
XLA Modules:
  0.0 40.7 jit_solution(12499954037724566052)
XLA Ops:
  0.6 37.2 %shard_map.94 = (f32[32,1024]{1,0:T(8,128)}, f32[32,1024]{1,0:T(8,128)}, f32[1,1024]{1,0:T(1,128)}) custom-call(bf16[256,1024]{1,0:T(8,128)(2,1)} %bitcast.7, bf16[1024,128]{1,0:T(8,128)(2,1)} %bitcast.8, bf16[128,1024]{1,0:T(8,128)(2,1)} %bitcast.9, bf16[1,1024]{1,0:T(2,128)(2,1)} %gain_ref.1, bf16[1024,128]{1,0:T(8,128)(2,1)} %head_ref.1, ...), custom_call_target="tpu_custom_call" | custom-call | tf_op jit(solution)/shard_map/pallas_call | solution.py:321
  37.8 0.0 copy-start
  37.8 1.6 %copy.13 = f32[1,1024,32]{1,2,0:T(8,128)} copy(f32[1,1024,32]{1,2,0:T(8,128)} %bitcast.11) | data formatting | bytes 262144
  39.4 0.0 copy-done
  39.4 0.0 copy-start.1
  39.4 0.7 %copy.14 = f32[1,32,1024]{2,1,0:T(8,128)} copy(f32[1,32,1024]{2,1,0:T(8,128)S(1)} %bitcast.10) | data formatting | bytes 262144
  40.1 0.0 copy-done.1
  40.1 0.6 %copy.15 = f32[1,1024]{1,0:T(1,128)} copy(f32[1,1024]{1,0:T(1,128)S(1)} %copy-done.1) | data formatting | bytes 8192
Async XLA Ops:
  37.8 1.6 %copy-start = (f32[32,1024]{1,0:T(8,128)S(1)}, f32[32,1024]{1,0:T(8,128)}, u32[]{:S(2)}) copy-start(f32[32,1024]{1,0:T(8,128)} %get-tuple-element.7) | copy-start | bytes 393220
  39.4 0.7 %copy-start.1 = (f32[1,1024]{1,0:T(1,128)S(1)}, f32[1,1024]{1,0:T(1,128)}, u32[]{:S(2)}) copy-start(f32[1,1024]{1,0:T(1,128)} %get-tuple-element.14) | copy-start | bytes 12292

commit v2 on v1

--- a/solution.py
+++ b/solution.py
@@ -32,10 +32,11 @@
 
 def kernel(
     nt, nd, width,
+    x_hbm, dn_hbm, up_hbm, gain_hbm, head_hbm, lab_hbm, val_hbm,
+    out,
     x_ref, dn_ref, up_ref, gain_ref, head_ref, lab_ref, val_ref,
-    down_out, up_out, gain_out,
     odn, oup, ogain, stok, rtok, sgram, rgram, pgram, gall, sres, res, sdp, rdp, sgn, rgn,
-    sib_s, sib_r, tok_s, tok_r, gr_s, gr_r, ga_s, ga_r, re_s, re_r, dp_s, dp_r,
+    load, sib_s, sib_r, tok_s, tok_r, gr_s, gr_r, ga_s, ga_r, re_s, re_r, fw_s, fw_r, dp_s, dp_r,
 ):
     s, d, t = lax.axis_index("section"), lax.axis_index("dp"), lax.axis_index("tensor")
     first = s == 0
@@ -52,12 +53,21 @@
 
     group = [(k, o) for k in range(nt) for o in (0, 1) if (k, o) != (0, 0)]
 
+    loads = [
+        pltpu.make_async_copy(a, b, load.at[i])
+        for i, (a, b) in enumerate((
+            (up_hbm, up_ref), (head_hbm, head_ref), (x_hbm, x_ref), (gain_hbm, gain_ref),
+            (dn_hbm, dn_ref), (lab_hbm, lab_ref), (val_hbm, val_ref),
+        ))
+    ]
+    for c in loads:
+        c.start()
+
     barrier = pltpu.get_barrier_semaphore()
     for k, o in group:
         pl.semaphore_signal(barrier, inc=1, device_id=peer(k, o), device_id_type=MESH)
     for k in range(1, nd):
         pl.semaphore_signal(barrier, inc=1, device_id=(s, lax.rem(d + k, nd), t), device_id_type=MESH)
-    pl.semaphore_wait(barrier, len(group) + nd - 1)
 
     def send(src, dst, ss, rs, to):
         copy = pltpu.make_async_remote_copy(
@@ -66,43 +76,69 @@
         copy.start()
         return copy
 
-    started = []
-    sib = [
-        send(a, b, sib_s.at[i], sib_r.at[i], peer(0, 1))
-        for i, (a, b) in enumerate(((up_ref, oup), (dn_ref, odn), (gain_ref, ogain)))
-    ]
-    started += sib
-
-    gain = gain_ref[...].astype(F32)
-    up = up_ref[...]
-    head = head_ref[...]
-    gram_a = mm_nt(up, up)
-    gram_b = mm(up, head)
-    sib[0].wait_recv()
-    gram_c = mm_nt(up, oup[...])
-    scaled_other = (oup[...].astype(F32) * gain).astype(BF16)
-    gram_d = mm(scaled_other, dn_ref[...])
-    gram_c = jnp.where(first, gram_c, gram_d)
-    for j, g in enumerate((gram_a, gram_b, gram_c)):
+    def put_gram(j, g):
         g = g.astype(wire)
         for i in range(nt):
             sgram[i, j] = g[i * rows : (i + 1) * rows]
-    gram_copies = []
-    for k in range(1, nt):
-        gram_copies.append(
-            send(sgram.at[lax.rem(t + k, nt)], rgram.at[k], gr_s.at[k], gr_r.at[k], peer(k, 0))
-        )
-    started += gram_copies
-
+
+    loads[0].wait()
+    up = up_ref[...]
+    put_gram(0, mm_nt(up, up))
+    loads[1].wait()
+    head = head_ref[...]
+    put_gram(1, mm(up, head))
+    for c in loads[2:]:
+        c.wait()
+    gain = gain_ref[...].astype(F32)
     xb = x_ref[...]
     xf = xb.astype(F32)
+    xup = mm_nt(xb, up).astype(wire)
     proj = mm((xf * gain).astype(BF16), dn_ref[...]).astype(wire)
-    xup = mm_nt(xb, up).astype(wire)
     for b in range(2):
         for i in range(nt):
             at = b * half + i * own
             stok[b, i, 0] = proj[at : at + own]
             stok[b, i, 1] = xup[at : at + own]
+
+    pl.semaphore_wait(barrier, len(group) + nd - 1)
+
+    sib = [
+        send(a, b, sib_s.at[i], sib_r.at[i], peer(0, 1))
+        for i, (a, b) in enumerate(((up_ref, oup), (dn_ref, odn), (gain_ref, ogain)))
+    ]
+    started = list(sib)
+    spans = (pl.ds(0, 2), pl.ds(2, 1))
+
+    def scatter_gram(j):
+        copies = [
+            send(
+                sgram.at[lax.rem(t + k, nt), spans[j]], rgram.at[k, spans[j]],
+                gr_s.at[j, k], gr_r.at[j, k], peer(k, 0),
+            )
+            for k in range(1, nt)
+        ]
+        started.extend(copies)
+        return copies
+
+    def gather_gram(j, copies):
+        total = sgram[t, spans[j]].astype(F32)
+        for k in range(1, nt):
+            copies[k - 1].wait_recv()
+            total = total + rgram[k, spans[j]].astype(F32)
+        total = total.astype(wire)
+        pgram[spans[j]] = total
+        gall[s, t, spans[j]] = total
+        out_copies = [
+            send(
+                pgram.at[spans[j]], gall.at[s, t, spans[j]],
+                ga_s.at[j, o, k], ga_r.at[j, o, k], peer(k, o),
+            )
+            for k, o in group
+        ]
+        started.extend(out_copies)
+        return out_copies
+
+    ab_copies = scatter_gram(0)
     tok_copies = {}
     for k in range(nt):
         to = lax.rem(t + k, nt)
@@ -123,24 +159,20 @@
         stok[s, i, 2] = hh[i * own : (i + 1) * own]
         stok[s, i, 3] = hl[i * own : (i + 1) * own]
         stok[s, i, 4] = q[i * own : (i + 1) * own]
+
+    sib[0].wait_recv()
+    gram_c = mm_nt(up, oup[...])
+    gram_d = mm((oup[...].astype(F32) * gain).astype(BF16), dn_ref[...])
+    put_gram(2, jnp.where(first, gram_c, gram_d))
+    c_copies = scatter_gram(1)
     for k in range(1, nt):
         to = lax.rem(t + k, nt)
         tok_copies[k, 0] = send(
             stok.at[s, to], rtok.at[0, k], tok_s.at[0, k], tok_r.at[0, k], peer(k, 0)
         )
     started += list(tok_copies.values())
-
-    total = sgram[t].astype(F32)
-    for k in range(1, nt):
-        gram_copies[k - 1].wait_recv()
-        total = total + rgram[k].astype(F32)
-    total = total.astype(wire)
-    pgram[...] = total
-    gall[s, t] = total
-    all_copies = [
-        send(pgram, gall.at[s, t], ga_s.at[o, k], ga_r.at[o, k], peer(k, o)) for k, o in group
-    ]
-    started += all_copies
+    all_copies = gather_gram(0, ab_copies)
+    all_copies = all_copies + gather_gram(1, c_copies)
 
     lab = jnp.where(first, lab_ref[0:1, :], lab_ref[1:2, :])
     val = jnp.where(first, val_ref[0:1, :], val_ref[1:2, :]).astype(F32)
@@ -230,24 +262,37 @@
         v = v.astype(wire)
         sres[j] = v
         res[s, t, j] = v
-    res_copies = [
-        send(sres, res.at[s, t], re_s.at[o, k], re_r.at[o, k], peer(k, o)) for k, o in group
-    ]
-    started += res_copies
+    res_copies = {
+        k: send(sres, res.at[s, t], re_s.at[k], re_r.at[k], peer(k, 0 if k else 1)) for k in range(nt)
+    }
+    forwards = []
+    for k in range(1, nt):
+        res_copies[k].wait_recv()
+        at = lax.rem(t + nt - k, nt)
+        forwards.append(send(res.at[s, at], res.at[s, at], fw_s.at[k], fw_r.at[k], peer(0, 1)))
+    started += list(res_copies.values()) + forwards
     sib[1].wait_recv()
     sib[2].wait_recv()
-    for c in res_copies:
+    res_copies[0].wait_recv()
+    for c in forwards:
         c.wait_recv()
 
     def got(j):
         return res[:, :, j].reshape(tokens, res.shape[-1])
-
-    dp_copies = []
 
     def piece(j, full):
         full = full.astype(BF16)
         for i in range(nd):
             sdp[i, j] = full[i * part : (i + 1) * part]
+        for k in range(1, nd):
+            dp_copy(j, k).start()
+
+    def dp_copy(j, k):
+        to = lax.rem(d + k, nd)
+        return pltpu.make_async_remote_copy(
+            src_ref=sdp.at[to, j], dst_ref=rdp.at[k, j], send_sem=dp_s.at[j, k], recv_sem=dp_r.at[j, k],
+            device_id=(s, to, t), device_id_type=MESH,
+        )
 
     def finish(state, own_w, own_h, cotangent):
         scaled = (state * gain).astype(BF16)
@@ -282,27 +327,33 @@
 
         finish(s1, w1g, h1g, cotangent)
 
+    small_copies = [
+        send(sgn, rgn.at[k], dp_s.at[2, k], dp_r.at[2, k], (s, lax.rem(d + k, nd), t)) for k in range(1, nd)
+    ]
+    started += small_copies
+    small = sgn[...]
     for k in range(1, nd):
-        to = (s, lax.rem(d + k, nd), t)
-        dp_copies.append((
-            send(sdp.at[lax.rem(d + k, nd)], rdp.at[k], dp_s.at[0, k], dp_r.at[0, k], to),
-            send(sgn, rgn.at[k], dp_s.at[1, k], dp_r.at[1, k], to),
-        ))
-    sums = sdp[d].astype(F32)
-    small = sgn[...]
-    for big, little in dp_copies:
-        started += [big, little]
-    for k in range(1, nd):
-        dp_copies[k - 1][1].wait_recv()
+        small_copies[k - 1].wait_recv()
         small = small + rgn[k]
-        dp_copies[k - 1][0].wait_recv()
-        sums = sums + rdp[k].astype(F32)
-    scale = 1.0 / small[1:2, :]
-    gain_out[...] = small[0:1, :] * scale
-    up_out[...] = sums[1] * scale
-    down_out[...] = sums[0] * scale
+    out[2 * part : 2 * part + 2, :] = small
+    for j in range(2):
+        sums = sdp[d, j].astype(F32)
+        for k in range(1, nd):
+            dp_copy(j, k).wait_recv()
+            sums = sums + rdp[k, j].astype(F32)
+        out[j * part : (j + 1) * part, :] = sums
+    for j in range(2):
+        for k in range(1, nd):
+            dp_copy(j, k).wait_send()
     for c in started:
         c.wait_send()
+
+
+def scale_kernel(part, sums, down_out, up_out, gain_out):
+    scale = 1.0 / sums[2 * part + 1 : 2 * part + 2, :]
+    down_out[...] = sums[0:part, :] * scale
+    up_out[...] = sums[part : 2 * part, :] * scale
+    gain_out[...] = sums[2 * part : 2 * part + 1, :] * scale
 
 
 def solution(mesh):
@@ -318,16 +369,20 @@
         wire = BF16 if own % 16 == 0 and rows % 16 == 0 else F32
         vmem = pl.BlockSpec(memory_space=pltpu.VMEM)
         dma = pltpu.SemaphoreType.DMA
-        down_t, up_g, gain_g = pl.pallas_call(
+        anyspace = pl.BlockSpec(memory_space=pl.ANY)
+        sums = pl.pallas_call(
             functools.partial(kernel, nt, nd, feats * nt),
-            out_shape=(
-                jax.ShapeDtypeStruct((part, feats), F32),
-                jax.ShapeDtypeStruct((part, feats), F32),
-                jax.ShapeDtypeStruct((1, feats), F32),
-            ),
-            in_specs=[vmem] * 7,
-            out_specs=(vmem,) * 3,
+            out_shape=jax.ShapeDtypeStruct((2 * part + 8, feats), F32),
+            in_specs=[anyspace] * 7,
+            out_specs=vmem,
             scratch_shapes=[
+                pltpu.VMEM((tokens, feats), BF16),
+                pltpu.VMEM((feats, rank), BF16),
+                pltpu.VMEM((rank, feats), BF16),
+                pltpu.VMEM((1, feats), BF16),
+                pltpu.VMEM((feats, head.shape[1]), BF16),
+                pltpu.VMEM((micro, per), jnp.int32),
+                pltpu.VMEM((micro, per), jnp.int32),
                 pltpu.VMEM((feats, rank), BF16),
                 pltpu.VMEM((rank, feats), BF16),
                 pltpu.VMEM((1, feats), BF16),
@@ -343,15 +398,27 @@
                 pltpu.VMEM((nd, 2, part, feats), BF16),
                 pltpu.VMEM((2, feats), F32),
                 pltpu.VMEM((nd, 2, feats), F32),
+                dma((7,)),
                 dma((3,)), dma((3,)),
                 dma((2, nt)), dma((2, nt)),
+                dma((2, nt)), dma((2, nt)),
+                dma((2, 2, nt)), dma((2, 2, nt)),
                 dma((nt,)), dma((nt,)),
-                dma((2, nt)), dma((2, nt)),
-                dma((2, nt)), dma((2, nt)),
-                dma((2, nd)), dma((2, nd)),
+                dma((nt,)), dma((nt,)),
+                dma((3, nd)), dma((3, nd)),
             ],
             compiler_params=pltpu.CompilerParams(collective_id=0, has_side_effects=True),
         )(inputs.reshape(tokens, feats), down[0], up[0], gains, head, labels, valid)
+        down_t, up_g, gain_g = pl.pallas_call(
+            functools.partial(scale_kernel, part),
+            out_shape=(
+                jax.ShapeDtypeStruct((part, feats), F32),
+                jax.ShapeDtypeStruct((part, feats), F32),
+                jax.ShapeDtypeStruct((1, feats), F32),
+            ),
+            in_specs=[vmem],
+            out_specs=(vmem,) * 3,
+        )(sums)
         return down_t.T[None], up_g[None], gain_g
 
     return jax.shard_map(

time: 40.9 us -> 37.8 us (0.924)
  local copies, waits for them, and re-layouts: 2.88 us -> 0 us
    unnamed x7 -> x0, local copies, waits for them, and re-layouts: 2.88 us -> none
    pallas_call x1 -> x2, Pallas kernels: 37.2 us -> 36.9 us  [the longest x1 35.2 us: local(): pl.pallas_call(functools.partial(kernel, nt, nd, feats * nt), out_shape=j...]
where the time goes in v2:
time: 37.8 us; the launch traced here: 37.5 us
  Pallas kernels  36.9 us (98%)
  between operations  0.64 us (2%)
    pallas_call x1, Pallas kernels, local(): pl.pallas_call(functools.partial(kernel, nt, nd, feats * nt), out_shape=j...  35.2 us
    pallas_call x1, Pallas kernels, local(): pl.pallas_call(functools.partial(scale_kernel, part), out_shape=(jax.Shap...  1.68 us

profile of v2, /device:TPU:0, one launch (start us, length us, event | category | flops | bytes accessed | tf_op | source)
XLA Modules:
  0.0 37.5 jit_solution(2613444083662344330)
XLA Ops:
  0.6 35.2 %shard_map.94.sums = f32[72,1024]{1,0:T(8,128)} custom-call(bf16[256,1024]{1,0:T(8,128)(2,1)} %bitcast.7, bf16[1024,128]{1,0:T(8,128)(2,1)} %bitcast.8, bf16[128,1024]{1,0:T(8,128)(2,1)} %bitcast.9, bf16[1,1024]{1,0:T(2,128)(2,1)} %gain_hbm.1, bf16[1024,128]{1,0:T(8,128)(2,1)} %head_hbm.1, s32[2,128]{1,0:T(2,128)} %lab_hbm.1, s32[2,128]{1,0:T(2,128)} %val_hbm.1), custom_call_target="tpu_custom_call" | custom-call | tf_op jit(solution)/shard_map/pallas_call | solution.py:373
  35.8 1.7 %shard_map.95 = (f32[32,1024]{1,0:T(8,128)}, f32[32,1024]{1,0:T(8,128)}, f32[1,1024]{1,0:T(1,128)}) custom-call(f32[72,1024]{1,0:T(8,128)} %shard_map.94.sums), custom_call_target="tpu_custom_call" | custom-call | tf_op jit(solution)/shard_map/pallas_call | solution.py:412

commit v3 on v2

--- a/solution.py
+++ b/solution.py
@@ -35,8 +35,8 @@
     x_hbm, dn_hbm, up_hbm, gain_hbm, head_hbm, lab_hbm, val_hbm,
     out,
     x_ref, dn_ref, up_ref, gain_ref, head_ref, lab_ref, val_ref,
-    odn, oup, ogain, stok, rtok, sgram, rgram, pgram, gall, sres, res, sdp, rdp, sgn, rgn,
-    load, sib_s, sib_r, tok_s, tok_r, gr_s, gr_r, ga_s, ga_r, re_s, re_r, fw_s, fw_r, dp_s, dp_r,
+    odn, oup, ogain, stok, rtok, sgram, rgram, pgram, gall, sres, res, sdp, rdp, rin, relay, psum, rcross, sgn, rgn,
+    load, sib_s, sib_r, tok_s, tok_r, gr_s, gr_r, ga_s, ga_r, re_s, re_r, fw_s, fw_r, dp_s, dp_r, rel_s, rel_r, cr_s, cr_r,
 ):
     s, d, t = lax.axis_index("section"), lax.axis_index("dp"), lax.axis_index("tensor")
     first = s == 0
@@ -284,23 +284,53 @@
         full = full.astype(BF16)
         for i in range(nd):
             sdp[i, j] = full[i * part : (i + 1) * part]
-        for k in range(1, nd):
-            dp_copy(j, k).start()
-
-    def dp_copy(j, k):
+
+    hl = nd // 2
+    side = d // hl
+    local_d = lax.rem(d, hl)
+    far = (1 - side) * hl
+    odd = lax.rem(d, 2)
+    outer = odd == side
+
+    def remote(src, dst, ss, rs, to):
+        return pltpu.make_async_remote_copy(
+            src_ref=src, dst_ref=dst, send_sem=ss, recv_sem=rs, device_id=(s, to, t), device_id_type=MESH
+        )
+
+    def up_copy(k):
         to = lax.rem(d + k, nd)
-        return pltpu.make_async_remote_copy(
-            src_ref=sdp.at[to, j], dst_ref=rdp.at[k, j], send_sem=dp_s.at[j, k], recv_sem=dp_r.at[j, k],
-            device_id=(s, to, t), device_id_type=MESH,
-        )
+        return remote(sdp.at[to, 1], rdp.at[k], dp_s.at[0, k], dp_r.at[0, k], to)
+
+    def near_copy(k):
+        to = side * hl + lax.rem(local_d + k, hl)
+        return remote(sdp.at[to, 0], rin.at[k], dp_s.at[1, k], dp_r.at[1, k], to)
+
+    def relay_copy():
+        return remote(sdp.at[pl.ds(far, hl), 0], relay, rel_s, rel_r, d + 1 - 2 * odd)
+
+    def cross_copy(i):
+        m = local_d // 2
+        return remote(psum.at[i], rcross.at[m], cr_s.at[i], cr_r.at[m], far + i)
+
+    def cross_wait(m):
+        return remote(psum.at[0], rcross.at[m], cr_s.at[0], cr_r.at[m], far)
 
     def finish(state, own_w, own_h, cotangent):
         scaled = (state * gain).astype(BF16)
         piece(0, mm_tn(own_w, scaled))
+
+        @pl.when(outer)
+        def _():
+            relay_copy().start()
+
         gain_row = jnp.sum(mm_nt(own_w, dn_ref[...]) * state, axis=0, keepdims=True)
         sgn[0:1, :] = gain_row
         sgn[1:2, :] = jnp.full((1, feats), count, F32)
         piece(1, mm_tn(own_h, cotangent().astype(BF16)))
+        for k in sorted(range(1, nd), key=lambda k: abs(k - hl)):
+            up_copy(k).start()
+        for k in range(1, hl):
+            near_copy(k).start()
 
     h0g, h1g, w1g, whg = (got(j).astype(BF16) for j in (0, 1, 3, 4))
     cg = got(5).astype(F32)
@@ -331,20 +361,46 @@
         send(sgn, rgn.at[k], dp_s.at[2, k], dp_r.at[2, k], (s, lax.rem(d + k, nd), t)) for k in range(1, nd)
     ]
     started += small_copies
+
+    @pl.when(jnp.logical_not(outer))
+    def _():
+        relay_copy().wait_recv()
+        psum[...] = (sdp[pl.ds(far, hl), 0].astype(F32) + relay[...].astype(F32)).astype(BF16)
+        for i in range(hl):
+            cross_copy(i).start()
+
     small = sgn[...]
     for k in range(1, nd):
         small_copies[k - 1].wait_recv()
         small = small + rgn[k]
     out[2 * part : 2 * part + 2, :] = small
-    for j in range(2):
-        sums = sdp[d, j].astype(F32)
-        for k in range(1, nd):
-            dp_copy(j, k).wait_recv()
-            sums = sums + rdp[k, j].astype(F32)
-        out[j * part : (j + 1) * part, :] = sums
-    for j in range(2):
-        for k in range(1, nd):
-            dp_copy(j, k).wait_send()
+    sums = sdp[d, 1].astype(F32)
+    for k in range(1, nd):
+        up_copy(k).wait_recv()
+        sums = sums + rdp[k].astype(F32)
+    out[part : 2 * part, :] = sums
+    sums = sdp[d, 0].astype(F32)
+    for k in range(1, hl):
+        near_copy(k).wait_recv()
+        sums = sums + rin[k].astype(F32)
+    for m in range(nd // 4):
+        cross_wait(m).wait_recv()
+        sums = sums + rcross[m].astype(F32)
+    out[0:part, :] = sums
+
+    @pl.when(outer)
+    def _():
+        relay_copy().wait_send()
+
+    @pl.when(jnp.logical_not(outer))
+    def _():
+        for i in range(hl):
+            cross_copy(i).wait_send()
+
+    for k in range(1, nd):
+        up_copy(k).wait_send()
+    for k in range(1, hl):
+        near_copy(k).wait_send()
     for c in started:
         c.wait_send()
 
@@ -358,7 +414,7 @@
 
 def solution(mesh):
     nt, nd, ns = mesh.shape["tensor"], mesh.shape["dp"], mesh.shape["section"]
-    assert ns == 2
+    assert ns == 2 and nd % 4 == 0
 
     def local(inputs, down, up, gains, head, labels, valid):
         micro, per, feats = inputs.shape
@@ -395,7 +451,11 @@
                 pltpu.VMEM((6, own, rank), wire),
                 pltpu.VMEM((2, nt, 6, own, rank), wire),
                 pltpu.VMEM((nd, 2, part, feats), BF16),
-                pltpu.VMEM((nd, 2, part, feats), BF16),
+                pltpu.VMEM((nd, part, feats), BF16),
+                pltpu.VMEM((nd // 2, part, feats), BF16),
+                pltpu.VMEM((nd // 2, part, feats), BF16),
+                pltpu.VMEM((nd // 2, part, feats), BF16),
+                pltpu.VMEM((nd // 4, part, feats), BF16),
                 pltpu.VMEM((2, feats), F32),
                 pltpu.VMEM((nd, 2, feats), F32),
                 dma((7,)),
@@ -406,6 +466,8 @@
                 dma((nt,)), dma((nt,)),
                 dma((nt,)), dma((nt,)),
                 dma((3, nd)), dma((3, nd)),
+                dma, dma,
+                dma((nd // 2,)), dma((nd // 4,)),
             ],
             compiler_params=pltpu.CompilerParams(collective_id=0, has_side_effects=True),
         )(inputs.reshape(tokens, feats), down[0], up[0], gains, head, labels, valid)

time: 37.8 us -> 35.9 us (0.950)
  Pallas kernels: 36.9 us -> 34.8 us
    pallas_call x1, Pallas kernels: 35.2 us -> 33.1 us  [local(): pl.pallas_call(functools.partial(kernel, nt, nd, feats * nt), out_shape=j...]
where the time goes in v3:
time: 35.9 us; the launch traced here: 35.4 us
  Pallas kernels  34.8 us (97%)
  between operations  0.64 us (2%)
    pallas_call x1, Pallas kernels, local(): pl.pallas_call(functools.partial(kernel, nt, nd, feats * nt), out_shape=j...  33.1 us
    pallas_call x1, Pallas kernels, local(): pl.pallas_call(functools.partial(scale_kernel, part), out_shape=(jax.Shap...  1.68 us

profile of v3, /device:TPU:0, one launch (start us, length us, event | category | flops | bytes accessed | tf_op | source)
XLA Modules:
  0.0 35.4 jit_solution(8925564569637848816)
XLA Ops:
  0.6 33.1 %shard_map.94.sums = f32[72,1024]{1,0:T(8,128)} custom-call(bf16[256,1024]{1,0:T(8,128)(2,1)} %bitcast.7, bf16[1024,128]{1,0:T(8,128)(2,1)} %bitcast.8, bf16[128,1024]{1,0:T(8,128)(2,1)} %bitcast.9, bf16[1,1024]{1,0:T(2,128)(2,1)} %gain_hbm.1, bf16[1024,128]{1,0:T(8,128)(2,1)} %head_hbm.1, s32[2,128]{1,0:T(2,128)} %lab_hbm.1, s32[2,128]{1,0:T(2,128)} %val_hbm.1), custom_call_target="tpu_custom_call" | custom-call | tf_op jit(solution)/shard_map/pallas_call | solution.py:429
  33.8 1.7 %shard_map.95 = (f32[32,1024]{1,0:T(8,128)}, f32[32,1024]{1,0:T(8,128)}, f32[1,1024]{1,0:T(1,128)}) custom-call(f32[72,1024]{1,0:T(8,128)} %shard_map.94.sums), custom_call_target="tpu_custom_call" | custom-call | tf_op jit(solution)/shard_map/pallas_call | solution.py:474
